TPU v7x, 256 devices: a whole 4x4x8 slice. The times are simulated.
256 devices in a mesh: fsdp: 32 (over y_lo, z, core), tp: 8 (over x, y_hi).
Axes of the slice: x: 4, y: 4 (y_hi: 2, y_lo: 2; y = y_hi * 2 + y_lo), z: 8, core: 2. Of those that a mesh axis runs over, the one named last changes fastest.
Arguments:
- hidden: bfloat16 [64, 5120], P(None, 'fsdp'), may hold values from -20 to 20
- query_weight: bfloat16 [5120, 5120], P(None, ('tp', 'fsdp')), may hold values from -0.078125 to 0.078125
- key_weight: bfloat16 [5120, 1024], P(None, ('tp', 'fsdp')), may hold values from -0.078125 to 0.078125
- value_weight: bfloat16 [5120, 1024], P(None, ('tp', 'fsdp')), may hold values from -0.078125 to 0.078125
- output_weight: bfloat16 [5120, 5120], P(('tp', 'fsdp')), may hold values from -0.078125 to 0.078125
- gate_weight: bfloat16 [5120, 27648], P(None, ('tp', 'fsdp')), may hold values from -0.078125 to 0.078125
- up_weight: bfloat16 [5120, 27648], P(None, ('tp', 'fsdp')), may hold values from -0.078125 to 0.078125
- down_weight: bfloat16 [27648, 5120], P(('tp', 'fsdp')), may hold values from -0.0390625 to 0.0390625
- history: float32 [7, 1024], replicated, may hold values from 0.0001 to 1, as said below
- slot: int32 [1], replicated, may hold values from 0 to 1023
- lengths: int32 [64], P('fsdp'), may hold values from 512 to 4096, as said below
- key_cache: bfloat16 [64, 4096, 1024], P('fsdp', None, 'tp'), may hold values from -1000 to 1000
- value_cache: bfloat16 [64, 4096, 1024], P('fsdp', None, 'tp'), may hold values from -6 to 6
Outputs:
- attention_out: bfloat16 [64, 5120], P('fsdp', 'tp')
- query_rollout: bfloat16 [5120, 5120], P('fsdp', 'tp')
- key_rollout: bfloat16 [5120, 1024], P('fsdp', 'tp')
- value_rollout: bfloat16 [5120, 1024], P('fsdp', 'tp')
- output_rollout: bfloat16 [5120, 5120], P('tp', 'fsdp')
- gate_rollout: bfloat16 [5120, 27648], P('fsdp', 'tp')
- up_rollout: bfloat16 [5120, 27648], P('fsdp', 'tp')
- down_rollout: bfloat16 [27648, 5120], P('tp', 'fsdp')
- new_history: float32 [7, 1024], replicated
Inputs may be any that keep to these rules, and one draw needn't show every extreme that they name: `history`: strictly positive. `lengths`: some sequence has all 4096 slots valid.
All inputs are finite; a program needn't handle non-finite values.
Results may differ from a plain program's by a relative error of at most 0.012.
The roundings to bfloat16 on the way count: a program that leaves them out, or rounds other values in their place, can miss the bound.
Values may be sent and summed in bfloat16 or wider, within the bound.
A program may use at most 64 MiB of HBM per device.

v0:
```python
import functools
import math

import jax
import jax.numpy as jnp
import numpy as np
from jax import lax
from jax.experimental import pallas as pl
from jax.experimental.pallas import tpu as pltpu
from jax.sharding import PartitionSpec as P

D = 5120
HEADS = 40
KV_HEADS = 8
HEAD_DIM = 128
GROUP = HEADS // KV_HEADS
CACHE = 4096
HIST = 1024
N = 32
TP = 8
ROWS = D // N
WIDE = 27648 // (N * TP)
SLIM = D // (N * TP)
TINY = KV_HEADS * HEAD_DIM // (N * TP)
LANES = 128
HEAD_COLS = LANES - SLIM - 2 * TINY
REST = WIDE - HEAD_COLS
CHUNK = 640
SPARE = LANES - WIDE - REST
TAIL = 16
SENT = ROWS - TAIL
MOVES = WIDE // SPARE
VMEM_LIMIT = 40 * 2**20

target_peak = 4.0
norm_eps = 1e-06
rope_theta = 1000000.0

F32 = jnp.float32
BF16 = jnp.bfloat16
MESH = pl.DeviceIdType.MESH


def offset(i):
    k = lax.div(i, 4) if isinstance(i, jax.Array) else i // 4
    odd = lax.rem(k, 2) if isinstance(i, jax.Array) else k % 2
    if isinstance(i, jax.Array):
        return lax.rem(lax.div(i, 2), 2), lax.rem(lax.div(k + 1, 2) * (2 * odd - 1) + 8, 8), lax.rem(i, 2)
    return (i // 2) % 2, ((k + 1) // 2 * (2 * odd - 1)) % 8, i % 2


def kernel(
    hid_h, wq_h, wk_h, wv_h, wo_h, wg_h, wu_h, wd_h, hist_h, slot, lens_h, kc_h, vc_h, spread_h,
    att_o, q_o, k_o, v_o, o_o, g_o, u_o, d_o, nh_o,
    wq, wk, wv, wo, wg, wu, wd, kc, vc, hid, hist, spread, lens, sent, got, fac,
    pk_s, pk_r, pt_s, pt_r, part, one_r, two_s, two_r,
    load_sem, send_sem, recv_sem, pks_sem, pkr_sem, pts_sem, ptr_sem,
    ones_sem, oner_sem, twos_sem, twor_sem, hop_sem,
    left_s, left_r, lfs_sem, lfr_sem,
):
    loads = [
        pltpu.make_async_copy(src, dst, load_sem.at[n])
        for n, (src, dst) in enumerate(
            [(wg_h, wg), (wq_h, wq), (wk_h, wk), (wv_h, wv), (wu_h, wu), (wd_h, wd), (wo_h, wo),
             (hid_h, hid), (hist_h, hist), (spread_h, spread), (lens_h, lens), (kc_h, kc), (vc_h, vc)]
        )
    ]
    for load in loads[:4]:
        load.start()

    me = lax.axis_index("fsdp")
    tp = lax.axis_index("tp")
    my_y, my_z, my_c = lax.div(me, 16), lax.rem(lax.div(me, 2), 8), lax.rem(me, 2)

    def device(dy, dz, dc):
        return lax.rem(my_y + dy, 2) * 16 + lax.rem(my_z + dz, 8) * 2 + lax.rem(my_c + dc, 2)

    def source(i):
        dy, dz, dc = offset(i)
        return device(dy, 8 - dz, dc)

    partners = [None] + [device(*offset(i)) for i in range(1, N)]
    near, middle, far = [*range(4, 12), *range(1, 4)], range(12, 20), range(20, N)

    barrier = pltpu.get_barrier_semaphore()
    for i in near:
        pl.semaphore_signal(barrier, 1, device_id={"fsdp": partners[i]}, device_id_type=MESH)
    for i in range(1, TP):
        pl.semaphore_signal(barrier, 1, device_id={"tp": lax.rem(tp + i, TP)}, device_id_type=MESH)

    shift = lax.rem(WIDE * me, LANES)

    def pack(tile, parts, chunk_of=lambda i: i, count=D // CHUNK):
        def body(i, _):
            cols = pl.ds(pl.multiple_of(chunk_of(i) * CHUNK, CHUNK), CHUNK)
            pieces = [ref[lo:hi, cols].astype(F32) for ref, lo, hi in parts]
            rows = sum(hi - lo for _, lo, hi in parts)
            if rows < LANES:
                pieces.append(jnp.zeros((LANES - rows, CHUNK), F32))
            block = jnp.concatenate(pieces, axis=0).T
            sent[tile, cols, :] = pltpu.roll(block, shift, 1).astype(BF16)
            return 0

        lax.fori_loop(0, count, body, 0)

    lane = lax.broadcasted_iota(jnp.int32, (1, LANES), 1)

    own_lanes = lax.div(lax.broadcasted_iota(jnp.int32, (TAIL, LANES), 1), REST) == lax.broadcasted_iota(
        jnp.int32, (TAIL, LANES), 0
    )

    tail_row = lax.broadcasted_iota(jnp.int32, (TAIL, LANES), 0)

    def slant(x, step):
        for bit in (1, 2, 4, 8):
            x = jnp.where(lax.rem(lax.div(tail_row, bit), 2) == 1, pltpu.roll(x, step * bit % LANES, 1), x)
        return x

    def fold(d, _):
        first = pl.multiple_of(d * ROWS, ROWS)
        tail = sent[1, pl.ds(pl.multiple_of(first + SENT, TAIL), TAIL), :].astype(F32)
        moved = jnp.concatenate([pltpu.roll(tail, WIDE + REST - SPARE * k, 1) for k in range(MOVES)], axis=0)
        free = lax.rem(lane - shift + LANES, LANES) >= WIDE + REST
        rows = pl.ds(first, SENT)
        sent[1, rows, :] = jnp.where(free, moved, sent[1, rows, :].astype(F32)).astype(BF16)
        turned = slant(pltpu.roll(tail, lax.rem(2 * LANES - WIDE - shift, LANES), 1), REST)
        left_s[d] = jnp.sum(jnp.where(own_lanes, turned, 0.0), axis=0, keepdims=True)
        return 0

    def unfold(block, left, s):
        x = block.astype(F32)
        base = lax.rem(WIDE * s, LANES)
        at = lax.rem(lane - base + LANES, LANES)
        spread_out = jnp.where(own_lanes, jnp.broadcast_to(left, (TAIL, LANES)), 0.0)
        tail = pltpu.roll(slant(spread_out, LANES - REST), lax.rem(WIDE + base, LANES), 1)
        for k in range(MOVES):
            piece = pltpu.roll(x[TAIL * k : TAIL * (k + 1), :], SPARE * (k + 1), 1)
            tail = jnp.where((at >= SPARE * k) & (at < SPARE * (k + 1)), piece, tail)
        return jnp.concatenate([x, tail], axis=0)

    def left_copy(to, slot_of, j=0):
        return pltpu.make_async_remote_copy(
            left_s.at[to], left_r.at[slot_of], lfs_sem.at[j], lfr_sem.at[slot_of], device_id={"fsdp": to}, device_id_type=MESH
        )

    def block_copy(tile, to, slot_of, j=0):
        return pltpu.make_async_remote_copy(
            sent.at[tile, pl.ds(pl.multiple_of(to * ROWS, ROWS), SENT if tile == 1 else ROWS)],
            got.at[tile, slot_of, pl.ds(0, SENT if tile == 1 else ROWS)],
            send_sem.at[tile, j],
            recv_sem.at[tile, slot_of],
            device_id={"fsdp": to},
            device_id_type=MESH,
        )

    def send(tile, order=range(N - 1, 0, -1)):
        for i in order:
            block_copy(tile, partners[i], me, i).start()

    for n in range(4):
        loads[n].wait()
    for load in loads[4:11]:
        load.start()
    first_tile = [(wg, 0, HEAD_COLS), (wq, 0, SLIM), (wk, 0, TINY), (wv, 0, TINY)]
    pair = lax.div(my_z, 2)
    beside = lax.rem(pair + 3 + 2 * lax.rem(my_z, 2), 4)

    def near_chunk(i):
        return lax.rem(i, 2) * 4 + pair + lax.div(i, 2) * (beside - pair)

    def far_chunk(i):
        return lax.rem(i, 2) * 4 + lax.rem(pair + lax.div(i, 2) * (beside - pair) + 2, 4)

    pack(0, first_tile, near_chunk, 4)
    pl.semaphore_wait(barrier, len(near) + TP - 1)

    def peak_copy(to, slot_of, j=0):
        return pltpu.make_async_remote_copy(
            pk_s, pk_r.at[slot_of], pks_sem.at[j], pkr_sem.at[slot_of], device_id={"fsdp": to}, device_id_type=MESH
        )

    def relay(sem, dz):
        for step in (dz, 8 - dz):
            pl.semaphore_signal(sem, 1, device_id={"fsdp": device(0, step, 0)}, device_id_type=MESH)

    relay(hop_sem.at[0], 1)
    send(0, near)

    for n in range(4, 7):
        loads[n].wait()

    mine = jnp.zeros((1, LANES), F32)
    for t, ref in enumerate((wq, wk, wv, wo, wg, wu, wd)):
        def body(c, best, ref=ref):
            cols = pl.ds(pl.multiple_of(c * CHUNK, CHUNK), CHUNK)
            return jnp.maximum(best, jnp.max(jnp.abs(ref[:, cols].astype(F32)), axis=0, keepdims=True))

        best = lax.fori_loop(0, D // CHUNK, body, jnp.zeros((1, CHUNK), F32))
        mine = jnp.where(lane == t, jnp.max(best, axis=1, keepdims=True), mine)
    pk_s[...] = mine

    def send_peaks(order):
        for i in order:
            peak_copy(partners[i], me, i).start()

    send_peaks(near)
    pack(0, first_tile, far_chunk, 4)
    pl.semaphore_wait(hop_sem.at[0], 2)
    relay(hop_sem.at[1], 2)
    send_peaks(middle)
    send(0, middle)
    pl.semaphore_wait(hop_sem.at[1], 2)
    send_peaks(far)
    send(0, far)
    for load in loads[11:]:
        load.start()
    pack(1, [(wu, 0, WIDE), (wg, HEAD_COLS, WIDE)])
    lax.fori_loop(0, N, fold, 0)
    for i in range(N - 1, 0, -1):
        left_copy(partners[i], me, i).start()
    send(1)

    def wait_peak(i, best):
        src = source(i)
        peak_copy(src, src).wait_recv()
        return jnp.maximum(best, pk_r[src])

    pt_s[...] = lax.fori_loop(1, N, wait_peak, mine)

    def tp_copy(to, slot_of, i=0):
        return pltpu.make_async_remote_copy(
            pt_s, pt_r.at[slot_of], pts_sem.at[i], ptr_sem.at[slot_of], device_id={"tp": to}, device_id_type=MESH
        )

    for i in range(1, TP):
        tp_copy(lax.rem(tp + i, TP), tp, i).start()
    pack(2, [(wd, 0, WIDE), (wo, 0, SLIM)])

    def wait_tp(i, best):
        src = lax.rem(tp + TP - i, TP)
        tp_copy(src, src).wait_recv()
        return jnp.maximum(best, pt_r[src])

    peaks = lax.fori_loop(1, TP, wait_tp, pt_s[...])

    for n in range(7, 11):
        loads[n].wait()
    on_row = lax.broadcasted_iota(jnp.int32, (7, LANES), 0) == lax.broadcasted_iota(jnp.int32, (7, LANES), 1)
    peaks_column = jnp.sum(jnp.where(on_row, peaks, 0.0), axis=1, keepdims=True)
    marked = lax.broadcasted_iota(jnp.int32, (7, HIST), 1) == slot[0]
    past = hist[...]
    kept = jnp.max(jnp.where(marked, 0.0, past), axis=1, keepdims=True)
    nh_o[...] = jnp.where(marked, peaks_column, past)
    fac[0:7, :] = jnp.broadcast_to(target_peak / jnp.maximum(peaks_column, kept), (7, LANES))

    def put(ref, tile, mask, value):
        cols = pl.ds(pl.multiple_of(tile * LANES, LANES), LANES)
        ref[:, cols] = jnp.where(mask, value, ref[:, cols].astype(F32)).astype(BF16)

    def place(ref, first, count, value):
        tiles = ref.shape[1] // LANES
        tile, at = lax.div(first, LANES), lax.rem(first, LANES)
        put(ref, tile, (lane >= at) & (lane < at + count), value)
        if tiles > 1:
            put(ref, tile + 1 - lax.div(tile + 1, tiles), lane < at + count - LANES, value)

    def turn(value, now, then):
        return pltpu.roll(value, lax.rem(then - now + 4 * LANES, LANES), 1)

    def process(tile, block, s):
        x = block.astype(F32)
        base = lax.rem(WIDE * s, LANES)
        if tile == 0:
            place(g_o, WIDE * s, HEAD_COLS, x * fac[4:5, :])
            place(q_o, SLIM * s, SLIM, turn(x * fac[0:1, :], base + HEAD_COLS, lax.rem(SLIM * s, LANES)))
            place(k_o, TINY * s, TINY, turn(x * fac[1:2, :], base + HEAD_COLS + SLIM, TINY * s))
            place(v_o, TINY * s, TINY, turn(x * fac[2:3, :], base + HEAD_COLS + SLIM + TINY, TINY * s))
        elif tile == 1:
            place(u_o, WIDE * s, WIDE, x * fac[5:6, :])
            place(g_o, WIDE * s + HEAD_COLS, REST, turn(x * fac[4:5, :], base + WIDE, lax.rem(WIDE * s + HEAD_COLS, LANES)))
        else:
            place(d_o, WIDE * s, WIDE, x * fac[6:7, :])
            place(o_o, SLIM * s, SLIM, turn(x * fac[3:4, :], base + WIDE, lax.rem(SLIM * s, LANES)))

    def receive(tile):
        process(tile, sent[tile, pl.ds(pl.multiple_of(me * ROWS, ROWS), ROWS), :], me)

        def body(j, _):
            src = source(1 + j if tile == 0 else N - 1 - j)
            block_copy(tile, src, src).wait_recv()
            if tile == 1:
                left_copy(src, src).wait_recv()
                process(tile, unfold(got[1, src, 0:SENT, :], left_r[src], src), src)
            else:
                process(tile, got[tile, src], src)
            return 0

        lax.fori_loop(0, N - 1, body, 0)

    receive(0)

    row = lax.broadcasted_iota(jnp.int32, (64, 64), 0)
    col = lax.broadcasted_iota(jnp.int32, (64, 64), 1)
    owner = (row // 32) * 32 + ((row // 2) % 8) * 4 + ((row // 16) % 2) * 2 + row % 2
    ordered = jnp.dot((owner == col).astype(BF16), hid[...], preferred_element_type=F32)
    hidden = ordered.astype(BF16)
    part[:, 0:640] = jnp.dot(hidden, q_o[...], preferred_element_type=F32)
    part[:, 640:768] = jnp.dot(hidden, k_o[...], preferred_element_type=F32)
    part[:, 768:896] = jnp.dot(hidden, v_o[...], preferred_element_type=F32)
    part[:, 896:1024] = jnp.broadcast_to(jnp.sum(ordered * ordered, axis=1, keepdims=True), (64, LANES))

    group = my_y * 2 + my_c

    def one_copy(k, receiving):
        y, c = lax.rem(my_y + k // 2, 2), lax.rem(my_c + k % 2, 2)
        other = y * 2 + c
        return other, pltpu.make_async_remote_copy(
            part.at[pl.ds(pl.multiple_of(other * 16, 16), 16)],
            one_r.at[other if receiving else group],
            ones_sem.at[other],
            oner_sem.at[other if receiving else group],
            device_id={"fsdp": y * 16 + my_z * 2 + c},
            device_id_type=MESH,
        )

    for k in range(1, 4):
        one_copy(k, False)[1].start()
    total = part[pl.ds(pl.multiple_of(group * 16, 16), 16), :]
    for k in range(1, 4):
        other, copy = one_copy(k, True)
        copy.wait_recv()
        total = total + one_r[other]
    for z in range(8):
        two_s[z] = total[2 * z : 2 * z + 2, :]

    def two_copy(z, slot_of, i=0):
        return pltpu.make_async_remote_copy(
            two_s.at[z],
            two_r.at[slot_of],
            twos_sem.at[i],
            twor_sem.at[slot_of],
            device_id={"fsdp": my_y * 16 + z * 2 + my_c},
            device_id_type=MESH,
        )

    for i in range(1, 8):
        two_copy(lax.rem(my_z + i, 8), my_z, i).start()
    send(2)
    receive(1)

    def wait_two(i, total):
        src = lax.rem(my_z + 8 - i, 8)
        two_copy(src, src).wait_recv()
        return total + two_r[src]

    summed = lax.fori_loop(1, 8, wait_two, two_s[my_z])

    inv_rms = lax.rsqrt(summed[:, 896:1024] / D + norm_eps)
    token = lax.broadcasted_iota(jnp.int32, (2, LANES), 0)
    length = jnp.where(token == 0, lens[0], lens[1])
    angle = length.astype(F32) * spread[...]
    half = lax.broadcasted_iota(jnp.int32, (2, LANES), 1) < HEAD_DIM // 2
    cosine = jnp.cos(angle)
    sine = jnp.where(half, -jnp.sin(angle), jnp.sin(angle))

    def rotate(x):
        return x * cosine + pltpu.roll(x, HEAD_DIM // 2, 1) * sine

    heads = [
        rotate(summed[:, h * LANES : (h + 1) * LANES] * inv_rms / fac[0:1, :]).astype(BF16).astype(F32)
        for h in range(GROUP)
    ]
    key_new = rotate(summed[:, 640:768] * inv_rms / fac[1:2, :]).astype(BF16).astype(F32)
    value_new = (summed[:, 768:896] * inv_rms / fac[2:3, :]).astype(BF16).astype(F32)
    loads[11].wait()
    loads[12].wait()
    head_row = lax.broadcasted_iota(jnp.int32, (8, LANES), 0)
    scale = HEAD_DIM ** (-0.5)
    mixes = []
    for b in range(2):
        query = jnp.zeros((8, LANES), F32)
        for h in range(GROUP):
            query = jnp.where(head_row == h, heads[h][b : b + 1, :], query)
        scores = (
            lax.dot_general(query.astype(BF16), kc[b], (((1,), (1,)), ((), ())), preferred_element_type=F32) * scale
        )
        own = jnp.sum(query * key_new[b : b + 1, :], axis=1, keepdims=True) * scale
        valid = lax.broadcasted_iota(jnp.int32, (8, CACHE), 1) < lens[b]
        top = jnp.maximum(jnp.max(jnp.where(valid, scores, -1e30), axis=1, keepdims=True), own)
        weights = jnp.where(valid, jnp.exp(scores - top), 0.0)
        own_weight = jnp.exp(own - top)
        total = jnp.sum(weights, axis=1, keepdims=True) + own_weight
        probs = (weights / total).astype(BF16)
        own_prob = (own_weight / total).astype(BF16).astype(F32)
        mixed = jnp.dot(probs, vc[b], preferred_element_type=F32)
        mixes.append(mixed + own_prob * value_new[b : b + 1, :])
    for h in range(GROUP):
        pair = jnp.where(token == 0, mixes[0][h : h + 1, :], mixes[1][h : h + 1, :])
        att_o[:, h * LANES : (h + 1) * LANES] = pair.astype(BF16)

    for i in range(1, N):
        peak_copy(partners[i], me, i).wait_send()
        left_copy(partners[i], me, i).wait_send()
        for tile in range(2):
            block_copy(tile, partners[i], me, i).wait_send()
    for i in range(1, TP):
        tp_copy(lax.rem(tp + i, TP), tp, i).wait_send()
    for k in range(1, 4):
        one_copy(k, False)[1].wait_send()
    for i in range(1, 8):
        two_copy(lax.rem(my_z + i, 8), my_z, i).wait_send()
    receive(2)
    for i in range(1, N):
        block_copy(2, partners[i], me, i).wait_send()


def finish(*refs):
    count = (len(refs) - 1) // 2
    copies = [pltpu.make_async_copy(refs[n], refs[count + n], refs[-1].at[n]) for n in range(count)]
    for copy in copies:
        copy.start()
    for copy in copies:
        copy.wait()


def per_device(
    hidden, query_weight, key_weight, value_weight, output_weight, gate_weight, up_weight, down_weight,
    history, slot, lengths, key_cache, value_cache,
):
    spread = np.float64(rope_theta) ** (-2.0 * (np.arange(HEAD_DIM) % (HEAD_DIM // 2)) / HEAD_DIM)
    spread = jnp.asarray(spread.astype(np.float32)[None, :])
    vmem = pl.BlockSpec(memory_space=pltpu.VMEM)
    hbm = pl.BlockSpec(memory_space=pltpu.HBM)
    out = [
        ((2, GROUP * HEAD_DIM), BF16),
        ((ROWS, 640), BF16),
        ((ROWS, 128), BF16),
        ((ROWS, 128), BF16),
        ((ROWS, 640), BF16),
        ((ROWS, 3456), BF16),
        ((ROWS, 3456), BF16),
        ((ROWS, 3456), BF16),
        ((7, HIST), F32),
    ]
    dma = pltpu.SemaphoreType.DMA
    results = pl.pallas_call(
        kernel,
        out_shape=[pltpu.VMEM(s, t) for s, t in out],
        in_specs=[hbm] * 9 + [pl.BlockSpec(memory_space=pltpu.SMEM)] + [hbm] * 4,
        out_specs=[vmem] * 9,
        scratch_shapes=[
            pltpu.VMEM((SLIM, D), BF16),
            pltpu.VMEM((TINY, D), BF16),
            pltpu.VMEM((TINY, D), BF16),
            pltpu.VMEM((SLIM, D), BF16),
            pltpu.VMEM((WIDE, D), BF16),
            pltpu.VMEM((WIDE, D), BF16),
            pltpu.VMEM((WIDE, D), BF16),
            pltpu.VMEM((2, CACHE, HEAD_DIM), BF16),
            pltpu.VMEM((2, CACHE, HEAD_DIM), BF16),
            pltpu.VMEM((64, ROWS), BF16),
            pltpu.VMEM((7, HIST), F32),
            pltpu.VMEM((1, LANES), F32),
            pltpu.SMEM((2,), jnp.int32),
            pltpu.VMEM((3, D, LANES), BF16),
            pltpu.VMEM((3, N, ROWS, LANES), BF16),
            pltpu.VMEM((8, LANES), F32),
            pltpu.VMEM((1, LANES), F32),
            pltpu.VMEM((N, 1, LANES), F32),
            pltpu.VMEM((1, LANES), F32),
            pltpu.VMEM((TP, 1, LANES), F32),
            pltpu.VMEM((64, 1024), F32),
            pltpu.VMEM((4, 16, 1024), F32),
            pltpu.VMEM((8, 2, 1024), F32),
            pltpu.VMEM((8, 2, 1024), F32),
            dma((13,)),
            dma((3, N)),
            dma((3, N)),
            dma((N,)),
            dma((N,)),
            dma((TP,)),
            dma((TP,)),
            dma((4,)),
            dma((4,)),
            dma((8,)),
            dma((8,)),
            pltpu.SemaphoreType.REGULAR((2,)),
            pltpu.VMEM((N, 1, LANES), F32),
            pltpu.VMEM((N, 1, LANES), F32),
            dma((N,)),
            dma((N,)),
        ],
        compiler_params=pltpu.CompilerParams(
            collective_id=0, has_side_effects=True, vmem_limit_bytes=VMEM_LIMIT
        ),
    )(
        *(
            x if x is slot else pltpu.with_memory_space_constraint(x, pltpu.HBM)
            for x in (
                hidden, query_weight.T, key_weight.T, value_weight.T, output_weight, gate_weight.T, up_weight.T,
                down_weight, history, slot, lengths, key_cache, value_cache, spread,
            )
        )
    )
    results = pl.pallas_call(
        finish,
        out_shape=[jax.ShapeDtypeStruct(s, t) for s, t in out],
        in_specs=[vmem] * 9,
        out_specs=[hbm] * 9,
        scratch_shapes=[dma((9,))],
        compiler_params=pltpu.CompilerParams(vmem_limit_bytes=8 * 2**20),
    )(*results)
    attention_out, query, key, value, output, gate, up, down, new_history = results
    return attention_out, query, key, value, output.T, gate, up, down.T, new_history


def solution(mesh):
    f, t = "fsdp", "tp"
    in_specs = (
        P(None, f), P(None, (t, f)), P(None, (t, f)), P(None, (t, f)), P((t, f), None), P(None, (t, f)),
        P(None, (t, f)), P((t, f), None), P(), P(), P(f), P(f, None, t), P(f, None, t),
    )
    out_specs = (P(f, t), P(f, t), P(f, t), P(f, t), P(t, f), P(f, t), P(f, t), P(t, f), P())
    return jax.shard_map(per_device, mesh=mesh, in_specs=in_specs, out_specs=out_specs, check_vma=False)
```

profile of v0, /device:TPU:1, one launch (start us, length us, event | category | flops | bytes accessed | tf_op | source)
XLA Modules:
  0.0 103.4 jit_solution(18284713933203218038)
XLA Ops:
  1.3 100.2 %shard_map.205 = (bf16[2,640]{1,0:T(2,128)(2,1)S(1)}, bf16[160,640]{1,0:T(8,128)(2,1)S(1)}, bf16[160,128]{1,0:T(8,128)(2,1)S(1)}, bf16[160,128]{1,0:T(8,128)(2,1...) custom-call(bf16[64,160]{1,0:T(8,128)(2,1)} %hid_h.1, ...), custom_call_target="tpu_custom_call" | custom-call | tf_op jit(solution)/shard_map/pallas_call | solution.py:446
  101.5 2.0 %shard_map.206 = (bf16[2,640]{1,0:T(2,128)(2,1)}, bf16[160,640]{1,0:T(8,128)(2,1)}, bf16[160,128]{1,0:T(8,128)(2,1)}, bf16[160,128]{1,0:T(8,128)(2,1)}, bf16[160...) custom-call(bf16[2,640]{1,0:T(2,128)(2,1)S(1)} %get-tuple-element.27, ...), custom_call_target="tpu_custom_call" | custom-call | tf_op jit(solution)/shard_map/pallas_call | solution.py:505
where the time goes:
time: 104 us; the launch traced here: 103 us
  Pallas kernels  102 us (98%)
  between operations  1.3 us (1%)
    pallas_call x1, Pallas kernels, per_device(): pl.pallas_call(kernel, out_shape=[pltpu.VMEM(s, t) for s, t in out], in_s...  100 us

commit v1 on v0

--- a/solution.py
+++ b/solution.py
@@ -197,6 +197,11 @@
 
         best = lax.fori_loop(0, D // CHUNK, body, jnp.zeros((1, CHUNK), F32))
         mine = jnp.where(lane == t, jnp.max(best, axis=1, keepdims=True), mine)
+    loads[7].wait()
+    features = hid[...].astype(F32)
+    squares = jnp.sum(features * features, axis=1, keepdims=True)
+    on_lane = lax.broadcasted_iota(jnp.int32, (64, LANES), 0) + 64 == lax.broadcasted_iota(jnp.int32, (64, LANES), 1)
+    mine = jnp.where(lane >= 64, jnp.sum(jnp.where(on_lane, squares, 0.0), axis=0, keepdims=True), mine)
     pk_s[...] = mine
 
     def send_peaks(order):
@@ -223,9 +228,10 @@
     def wait_peak(i, best):
         src = source(i)
         peak_copy(src, src).wait_recv()
-        return jnp.maximum(best, pk_r[src])
-
-    pt_s[...] = lax.fori_loop(1, N, wait_peak, mine)
+        return jnp.where(lane >= 64, best + pk_r[src], jnp.maximum(best, pk_r[src]))
+
+    over_fsdp = lax.fori_loop(1, N, wait_peak, mine)
+    pt_s[...] = over_fsdp
 
     def tp_copy(to, slot_of, i=0):
         return pltpu.make_async_remote_copy(
@@ -243,7 +249,7 @@
 
     peaks = lax.fori_loop(1, TP, wait_tp, pt_s[...])
 
-    for n in range(7, 11):
+    for n in range(8, 11):
         loads[n].wait()
     on_row = lax.broadcasted_iota(jnp.int32, (7, LANES), 0) == lax.broadcasted_iota(jnp.int32, (7, LANES), 1)
     peaks_column = jnp.sum(jnp.where(on_row, peaks, 0.0), axis=1, keepdims=True)
@@ -307,7 +313,6 @@
     part[:, 0:640] = jnp.dot(hidden, q_o[...], preferred_element_type=F32)
     part[:, 640:768] = jnp.dot(hidden, k_o[...], preferred_element_type=F32)
     part[:, 768:896] = jnp.dot(hidden, v_o[...], preferred_element_type=F32)
-    part[:, 896:1024] = jnp.broadcast_to(jnp.sum(ordered * ordered, axis=1, keepdims=True), (64, LANES))
 
     group = my_y * 2 + my_c
 
@@ -355,8 +360,9 @@
 
     summed = lax.fori_loop(1, 8, wait_two, two_s[my_z])
 
-    inv_rms = lax.rsqrt(summed[:, 896:1024] / D + norm_eps)
     token = lax.broadcasted_iota(jnp.int32, (2, LANES), 0)
+    own_squares = jnp.where(lane == 64 + 2 * me + token, jnp.broadcast_to(over_fsdp, (2, LANES)), 0.0)
+    inv_rms = lax.rsqrt(jnp.sum(own_squares, axis=1, keepdims=True) / D + norm_eps)
     length = jnp.where(token == 0, lens[0], lens[1])
     angle = length.astype(F32) * spread[...]
     half = lax.broadcasted_iota(jnp.int32, (2, LANES), 1) < HEAD_DIM // 2
@@ -469,10 +475,10 @@
             pltpu.VMEM((N, 1, LANES), F32),
             pltpu.VMEM((1, LANES), F32),
             pltpu.VMEM((TP, 1, LANES), F32),
-            pltpu.VMEM((64, 1024), F32),
-            pltpu.VMEM((4, 16, 1024), F32),
-            pltpu.VMEM((8, 2, 1024), F32),
-            pltpu.VMEM((8, 2, 1024), F32),
+            pltpu.VMEM((64, 896), F32),
+            pltpu.VMEM((4, 16, 896), F32),
+            pltpu.VMEM((8, 2, 896), F32),
+            pltpu.VMEM((8, 2, 896), F32),
             dma((13,)),
             dma((3, N)),
             dma((3, N)),

time: 104 us -> 103 us (level)
  no operation moved by 1% of the time
where the time goes in v1:
time: 103 us
  Pallas kernels  102 us (99%)
  between operations  1.3 us (1%)
    pallas_call x1, Pallas kernels, per_device(): pl.pallas_call(kernel, out_shape=[pltpu.VMEM(s, t) for s, t in out], in_s...  100 us

profile of v1, /device:TPU:1, one launch (start us, length us, event | category | flops | bytes accessed | tf_op | source)
XLA Modules:
  0.0 103.3 jit_solution(11825534875686273026)
XLA Ops:
  1.3 100.0 %shard_map.205 = (bf16[2,640]{1,0:T(2,128)(2,1)S(1)}, bf16[160,640]{1,0:T(8,128)(2,1)S(1)}, bf16[160,128]{1,0:T(8,128)(2,1)S(1)}, bf16[160,128]{1,0:T(8,128)(2,1...) custom-call(bf16[64,160]{1,0:T(8,128)(2,1)} %hid_h.1, ...), custom_call_target="tpu_custom_call" | custom-call | tf_op jit(solution)/shard_map/pallas_call | solution.py:452
  101.3 2.0 %shard_map.206 = (bf16[2,640]{1,0:T(2,128)(2,1)}, bf16[160,640]{1,0:T(8,128)(2,1)}, bf16[160,128]{1,0:T(8,128)(2,1)}, bf16[160,128]{1,0:T(8,128)(2,1)}, bf16[160...) custom-call(bf16[2,640]{1,0:T(2,128)(2,1)S(1)} %get-tuple-element.27, ...), custom_call_target="tpu_custom_call" | custom-call | tf_op jit(solution)/shard_map/pallas_call | solution.py:511
